TPU v7x, 8 devices: a whole 2x2x1 slice. The times are simulated.
8 devices in a mesh: fsdp: 2 (over z, y), tp: 4 (over x, core).
Axes of the slice: x: 2, y: 2, z: 1, core: 2. Of those that a mesh axis runs over, the one named last changes fastest.
Arguments:
- x_in: bfloat16 [256, 256, 1024], P('fsdp')
- seq_lens: int32 [256], P('fsdp')
- grad_out: bfloat16 [256, 256, 1024], P('fsdp')
- ln1_gain: bfloat16 [1024], P('fsdp')
- ln1_bias: bfloat16 [1024], P('fsdp')
- w_query: bfloat16 [1024, 16, 64], P('fsdp', 'tp')
- b_query: bfloat16 [1024], P(('tp', 'fsdp'))
- w_key: bfloat16 [1024, 16, 64], P('fsdp', 'tp')
- b_key: bfloat16 [1024], P(('tp', 'fsdp'))
- w_value: bfloat16 [1024, 16, 64], P('fsdp', 'tp')
- b_value: bfloat16 [1024], P(('tp', 'fsdp'))
- w_out: bfloat16 [16, 64, 1024], P('tp', None, 'fsdp')
- b_out: bfloat16 [1024], P('fsdp')
- ln2_gain: bfloat16 [1024], P('fsdp')
- ln2_bias: bfloat16 [1024], P('fsdp')
- w_fc1: bfloat16 [1024, 4096], P('fsdp', 'tp')
- b_fc1: bfloat16 [4096], P(('tp', 'fsdp'))
- w_fc2: bfloat16 [4096, 1024], P('tp', 'fsdp')
- b_fc2: bfloat16 [1024], P('fsdp')
Outputs:
- output 1: bfloat16 [256, 256, 1024], P('fsdp')
- output 2: bfloat16 [256, 256, 1024], P('fsdp')
- output 3: float32 [1024], P('fsdp')
- output 4: float32 [1024], P('fsdp')
- output 5: float32 [1024, 16, 64], P('fsdp', 'tp')
- output 6: float32 [1024], P(('tp', 'fsdp'))
- output 7: float32 [1024, 16, 64], P('fsdp', 'tp')
- output 8: float32 [1024], P(('tp', 'fsdp'))
- output 9: float32 [1024, 16, 64], P('fsdp', 'tp')
- output 10: float32 [1024], P(('tp', 'fsdp'))
- output 11: float32 [16, 64, 1024], P('tp', None, 'fsdp')
- output 12: float32 [1024], P('fsdp')
- output 13: float32 [1024], P('fsdp')
- output 14: float32 [1024], P('fsdp')
- output 15: float32 [1024, 4096], P('fsdp', 'tp')
- output 16: float32 [4096], P(('tp', 'fsdp'))
- output 17: float32 [4096, 1024], P('tp', 'fsdp')
- output 18: float32 [1024], P('fsdp')
All inputs are finite; a program needn't handle non-finite values.
Results may differ from a plain program's by a relative error of at most 0.0164221.
Values are sent between devices in bfloat16 or wider.
A program may use at most 1.25 GiB of HBM per device.

v0:
```python
import functools

import jax
import jax.numpy as jnp
from jax import lax
from jax.experimental import pallas as pl
from jax.experimental.pallas import tpu as pltpu
from jax.sharding import PartitionSpec as P


F32 = jnp.float32
BF16 = jnp.bfloat16
LN_EPS = 1e-5
ROPE_BASE = 10000.0
MASKED = -1e30
D = 1024
HEADS = 16
HEAD = 64
FF = 4096
L = 256
LANES = 128
TP = 4
FSDP = 2
CHUNKS = 4
SWAP = [(0, 1), (1, 0)]
VMEM_LIMIT = 67043328
ROWS, SPLIT = P('fsdp'), P(('x', 'core', 'fsdp'))
HEADS_IN, HEADS_OUT = P('fsdp', ('x', 'core'), None), P(('x', 'core'), None, 'fsdp')
PARAM_SPECS = dict(ln1_gain=ROWS, ln1_bias=ROWS, w_query=HEADS_IN, b_query=SPLIT, w_key=HEADS_IN, b_key=SPLIT, w_value=HEADS_IN, b_value=SPLIT,
                   w_out=HEADS_OUT, b_out=ROWS, ln2_gain=ROWS, ln2_bias=ROWS, w_fc1=P('fsdp', ('x', 'core')), b_fc1=SPLIT,
                   w_fc2=P(('x', 'core'), 'fsdp'), b_fc2=ROWS)
PARAM_NAMES = tuple(PARAM_SPECS)
FSDP_VECTORS = tuple(name for name, spec in PARAM_SPECS.items() if spec is ROWS)
BOTH_VECTORS = tuple(name for name, spec in PARAM_SPECS.items() if spec is SPLIT)
BOTH = ('x', 'core', 'fsdp')

ERF_P = 0.3275911 * 0.7071067811865476
ERF_C = (0.254829592, -0.284496736, 1.421413741, -1.453152027, 1.061405429)
LOG2E = 1.4426950408889634
INV_SQRT_2PI = 0.3989422804014327


def nn(lhs, rhs):
    return lax.dot_general(lhs, rhs, (((1,), (0,)), ((), ())), preferred_element_type=F32)


def nt(lhs, rhs):
    return lax.dot_general(lhs, rhs, (((1,), (1,)), ((), ())), preferred_element_type=F32)


def tn(lhs, rhs):
    return lax.dot_general(lhs, rhs, (((0,), (0,)), ((), ())), preferred_element_type=F32)


def sum_groups(values):
    return values.reshape(values.shape[0] // 8, 8, values.shape[1]).sum(axis=0)


def standardize(values):
    centered = values - jnp.mean(values, axis=-1, keepdims=True)
    rstd = lax.rsqrt(jnp.mean(centered * centered, axis=-1, keepdims=True) + LN_EPS)
    return centered * rstd, rstd


def norm_input_grad(d_norm, gain, xhat, rstd):
    scaled = d_norm * gain
    mean_scaled = jnp.mean(scaled, axis=-1, keepdims=True)
    mean_dot = jnp.mean(scaled * xhat, axis=-1, keepdims=True)
    return rstd * (scaled - mean_scaled - xhat * mean_dot)


def gelu_and_grad(pre_act, d_act):
    t = 1.0 / (1.0 + ERF_P * jnp.abs(pre_act))
    gauss = jnp.exp2((-0.5 * LOG2E) * (pre_act * pre_act))
    poly = 0.5 * ERF_C[4]
    for coef in reversed(ERF_C[:4]):
        poly = poly * t + 0.5 * coef
    tail = poly * t * gauss
    cdf = jnp.where(pre_act < 0, tail, 1.0 - tail)
    slope = cdf + pre_act * (gauss * INV_SQRT_2PI)
    return pre_act * cdf, d_act * slope


def rope_tables():
    inv_freq = ROPE_BASE ** (-jnp.arange(0, HEAD, 2, dtype=F32) / HEAD)
    angles = jnp.arange(L, dtype=F32)[:, None] * inv_freq[None, :]
    cos, sin = jnp.cos(angles), jnp.sin(angles)
    wide_cos = jnp.concatenate([cos] * 4, axis=-1)
    wide_sin = jnp.concatenate([-sin, sin, -sin, sin], axis=-1)
    return wide_cos, wide_sin, cos.T, sin.T


def swap_halves(values):
    lane = lax.broadcasted_iota(jnp.int32, values.shape, 1)
    return jnp.where(lane % HEAD < HEAD // 2, pltpu.roll(values, LANES - HEAD // 2, 1), pltpu.roll(values, HEAD // 2, 1))


def only_head(tile, head):
    lane = lax.broadcasted_iota(jnp.int32, tile.shape, 1)
    return jnp.where((lane >= HEAD) == (head % 2 == 1), tile, jnp.zeros_like(tile))


def pair_lanes(head, base=0):
    first = base + head // 2 * LANES
    return slice(first, first + LANES)


def attn_fwd_body(seq_of, ready, meta, lens, x, b, gain, bias, cos, sin, w, h1_out, q_out, k_out, v_out, ctx_out, stats_out):
    seq_len = lens[seq_of(pl.program_id(0), meta)]
    xhat, _ = standardize(x[...].astype(F32))
    h1 = (xhat * gain[...] + bias[...]).astype(BF16)
    h1_out[...] = h1
    ready(0)
    for part, out in enumerate((q_out, k_out)):
        lin = nn(h1, w[:, part * D:(part + 1) * D]) + b[:, part * D:(part + 1) * D]
        for pair in range(D // LANES):
            lanes = slice(pair * LANES, (pair + 1) * LANES)
            tile = lin[:, lanes] * HEAD ** -0.5 if part == 0 else lin[:, lanes]
            out[:, lanes] = (tile * cos[...] + swap_halves(tile) * sin[...]).astype(BF16)
    v_out[...] = (nn(h1, w[:, 2 * D:]) + b[:, 2 * D:]).astype(BF16)
    key_ok = lax.broadcasted_iota(jnp.int32, (L, L), 1) < seq_len

    def scores_of(head):
        return nt(only_head(q_out[:, pair_lanes(head)], head), k_out[:, pair_lanes(head)])

    ahead = 2
    scores = [scores_of(head) for head in range(ahead)]
    lane = lax.broadcasted_iota(jnp.int32, (L, LANES), 1)
    stats = jnp.zeros((L, LANES), F32)
    ctx = None
    for head in range(HEADS):
        if head + ahead < HEADS:
            scores.append(scores_of(head + ahead))
        masked = jnp.where(key_ok, scores[head], MASKED)
        scores[head] = None
        top = jnp.max(masked, axis=1, keepdims=True)
        weights = jnp.exp(masked - top)
        total = jnp.sum(weights, axis=1, keepdims=True)
        inverse = 1.0 / total
        stats = jnp.where(lane == head, top, jnp.where(lane == HEADS + head, inverse, stats))
        part = nn((weights * inverse).astype(BF16), only_head(v_out[:, pair_lanes(head)], head))
        ctx = part if head % 2 == 0 else ctx + part
        if head % 2 == 1:
            ctx_out[:, pair_lanes(head)] = ctx.astype(BF16)
    stats_out[0] = stats.T[:2 * HEADS]


def mlp_body(ready, meta, x, ctx, dy, bo, gain, bias, b1, b2, rows_in, cols_in, wo, w1, w2, y_out, da_out, dctx_out, h2_out, act_out, du_out, dab_out, row_sums, col_sums):
    cols = D

    @pl.when(pl.program_id(0) == 0)
    def _():
        row_sums[...] = rows_in[...]
        col_sums[...] = cols_in[...]

    ready(0)
    resid = (x[...].astype(F32) + nn(ctx[...], wo[...]) + bo[...]).astype(BF16).astype(F32)
    xhat, rstd = standardize(resid)
    h2 = (xhat * gain[...] + bias[...]).astype(BF16)
    h2_out[...] = h2
    ready(1)
    ready(2)
    y_acc = jnp.zeros((L, D), F32)
    dh_acc = jnp.zeros((L, D), F32)
    for step in range(FF // cols):
        sl = slice(step * cols, (step + 1) * cols)
        pre_act = nn(h2, w1[:, sl]) + b1[:, sl]
        act, du = gelu_and_grad(pre_act, nt(dy[...], w2[sl, :]))
        col_sums[:, sl] += sum_groups(du)
        act, du = act.astype(BF16), du.astype(BF16)
        act_out[:, sl] = act
        du_out[:, sl] = du
        y_acc += nn(act, w2[sl, :])
        dh_acc += nt(du, w1[:, sl])
    y_out[...] = (resid + y_acc + b2[...]).astype(BF16)
    dy_f32 = dy[...].astype(F32)
    da = norm_input_grad(dh_acc, gain[...], xhat, rstd) + dy_f32
    da_out[...] = da
    da_b = da.astype(BF16)
    dab_out[...] = da_b
    dctx_out[...] = nt(da_b, wo[...]).astype(BF16)
    row_sums[0] += sum_groups(dh_acc * xhat)
    row_sums[1] += sum_groups(dh_acc)
    row_sums[2] += sum_groups(da)
    row_sums[3] += sum_groups(dy_f32)


def attn_bwd_body(ready, meta, lens, x, q, k, v, dctx, stats, da, gain, cos, sin, cos_t, sin_t, rows_in, q_in, kv_in, w, dx_out, dqkv_out, row_sums, q_sums, kv_sums, k_t, dq_t):
    @pl.when(pl.program_id(0) == 0)
    def _():
        row_sums[...] = rows_in[...]
        q_sums[...] = q_in[...]
        kv_sums[...] = kv_in[...]

    seq_len = lens[meta[0] + pl.program_id(0)]
    k_t[...] = k[...].T
    key_ok = lax.broadcasted_iota(jnp.int32, (L, L), 0) < seq_len
    half = HEAD // 2

    def products(head):
        lanes = pair_lanes(head)
        return nt(only_head(k[:, lanes], head), q[:, lanes]), nt(only_head(v[:, lanes], head), dctx[:, lanes])

    def softmax_grad(head, scores, d_probs):
        probs = jnp.exp(jnp.where(key_ok, scores, MASKED) - stats[0, head:head + 1, :]) * stats[0, HEADS + head:HEADS + head + 1, :]
        d_scores = probs * (d_probs - jnp.sum(d_probs * probs, axis=0, keepdims=True))
        return probs.astype(BF16), d_scores.astype(BF16)

    pending = {}

    def gradients(head, probs, d_scores):
        lanes = pair_lanes(head)
        dv = nn(probs, only_head(dctx[:, lanes], head))
        dk = nn(d_scores, only_head(q[:, lanes], head))
        dq = nn(k_t[head * HEAD:(head + 1) * HEAD, :], d_scores)
        low = (dq[:half] * cos_t[...] + dq[half:] * sin_t[...]) * HEAD ** -0.5
        high = (dq[half:] * cos_t[...] - dq[:half] * sin_t[...]) * HEAD ** -0.5
        for first, part in ((head * HEAD, low), (head * HEAD + half, high)):
            rows = slice(first, first + half)
            q_sums[rows, :] += part[:, :LANES] + part[:, LANES:]
            dq_t[rows, :] = part.astype(BF16)
        if head % 2 == 0:
            pending[head // 2] = dv, dk
            return
        dv_first, dk_first = pending.pop(head // 2)
        dv, dk = dv_first + dv, dk_first + dk
        dk = dk * cos[...] - swap_halves(dk) * sin[...]
        kv_sums[0, :, lanes] += sum_groups(dk)
        kv_sums[1, :, lanes] += sum_groups(dv)
        dqkv_out[:, pair_lanes(head, D)] = dk.astype(BF16)
        dqkv_out[:, pair_lanes(head, 2 * D)] = dv.astype(BF16)

    ahead = 2
    first = [products(head) for head in range(ahead)]
    second = None
    for head in range(HEADS):
        if head + ahead < HEADS:
            first.append(products(head + ahead))
        if second is not None:
            gradients(head - 1, *second)
        second = softmax_grad(head, *first[head])
        first[head] = None
    gradients(HEADS - 1, *second)
    dqkv_out[:, :D] = dq_t[...].T
    ready(0)
    dh = nt(dqkv_out[...], w[...])
    xhat, rstd = standardize(x[...].astype(F32))
    dx_out[...] = (da[...] + norm_input_grad(dh, gain[...], xhat, rstd)).astype(BF16)
    row_sums[0] += sum_groups(dh * xhat)
    row_sums[1] += sum_groups(dh)


def weight_grad_body(store, meta, lhs, rhs, *rest):
    partner, out = rest if len(rest) == 2 else (None, rest[0])
    acc = tn(lhs[...], rhs[...])
    k_step = pl.program_id(1)

    @pl.when(k_step == 0)
    def _():
        for at, part in store(acc):
            out[at] = part if partner is None else part + partner[at]

    @pl.when(k_step > 0)
    def _():
        for at, part in store(acc):
            out[at] += part


class Placing:
    def __init__(self, pieces, target, chunk):
        self.pieces, self.target, self.chunk = pieces, target, chunk

    def moves(self, steps):
        return 1 << (steps.bit_length() - 1)

    def rows_per_step(self, steps):
        return self.pieces[0].shape[0] // self.moves(steps)

    def scratch(self, steps):
        n = len(self.pieces)
        return [pltpu.VMEM((2, n, self.rows_per_step(steps), D), BF16), pltpu.SemaphoreType.DMA((2, n)), pltpu.SemaphoreType.DMA((2, n))]

    def hooks(self, steps, step, meta, pieces, target, buf, in_sem, out_sem):
        rows = self.rows_per_step(steps)
        total = self.pieces[0].shape[0]

        def fetch(j, s):
            return pltpu.make_async_copy(pieces[j].at[pl.ds(s * rows, rows)], buf.at[s % 2, j], in_sem.at[s % 2, j])

        def put(j, s):
            row = pl.multiple_of((meta[3] * TP + jnp.bitwise_xor(meta[1], j)) * total + s * rows, rows)
            return pltpu.make_async_copy(buf.at[s % 2, j], target.at[pl.ds(row, rows)], out_sem.at[s % 2, j])

        every = range(len(self.pieces))
        moves = self.moves(steps)

        def before():
            @pl.when((step >= 2) & (step < moves))
            def _():
                for j in every:
                    put(j, step - 2).wait()

            @pl.when(step < moves)
            def _():
                for j in every:
                    fetch(j, step).start()

        def after():
            @pl.when(step < moves)
            def _():
                for j in every:
                    fetch(j, step).wait()
                    put(j, step).start()

            @pl.when(step == moves - 1)
            def _():
                for j in every:
                    put(j, step - 1).wait()
                    put(j, step).wait()

        return before, after


def call(body, grid, scalars, streams, consts, weights, outs, prior, scratch, flops, n_bytes, placing=None, hand_on=False):
    steps = 1
    for size in grid:
        steps *= size

    def whole(array):
        return pl.BlockSpec(array.shape, lambda *_: (0,) * array.ndim, pipeline_mode=pl.Buffered(1))

    anywhere = pl.BlockSpec(memory_space=pl.ANY)
    n_scalar, n_stream, n_const, n_weight, n_out = len(scalars), len(streams), len(consts), len(weights), len(outs)
    operands = [a for a, _, _ in streams] + list(consts) + [a for a, _, _ in weights] + list(prior.values())
    in_specs = [pl.BlockSpec(block, index) for _, block, index in streams] + [whole(a) for a in consts] + [anywhere] * (n_weight + len(prior))
    aliases = {n_scalar + n_stream + n_const + n_weight + i: out for i, out in enumerate(prior)}
    out_specs = [pl.BlockSpec(block, index) for _, _, block, index in outs]
    out_shape = [jax.ShapeDtypeStruct(shape, dtype) for shape, dtype, _, _ in outs]
    n_hand = n_weight if hand_on else 0
    n_piece = 0
    scratches = [pltpu.VMEM(shape, BF16) for _, shape, _ in weights] + [pltpu.SemaphoreType.DMA((len(moves),)) for _, _, moves in weights]
    if placing is not None:
        n_piece = len(placing.pieces)
        aliases[n_scalar + len(operands) + n_piece] = n_out
        operands += list(placing.pieces) + [placing.target]
        in_specs += [anywhere] * (n_piece + 1)
        out_specs.append(anywhere)
        out_shape.append(jax.ShapeDtypeStruct(placing.target.shape, placing.target.dtype))
        scratches += placing.scratch(steps)
    out_specs += [anywhere] * n_hand
    out_shape += [jax.ShapeDtypeStruct(shape, BF16) for _, shape, _ in weights[:n_hand]]
    scratches += [pltpu.SemaphoreType.DMA((n_hand,))] * bool(n_hand) + scratch

    def kernel(*refs):
        refs = list(refs)

        def take(n):
            taken = refs[:n]
            del refs[:n]
            return taken

        scalar_refs, stream_refs, const_refs, weight_refs = take(n_scalar), take(n_stream), take(n_const), take(n_weight)
        take(len(prior))
        piece_refs = take(n_piece)
        if placing is not None:
            take(1)
        out_refs = take(n_out)
        target = take(1) if placing is not None else None
        handed = take(n_hand)
        held, sems = take(n_weight), take(n_weight)
        step = pl.program_id(0)
        for axis in range(1, len(grid)):
            step = step * grid[axis] + pl.program_id(axis)

        copies = [[pltpu.make_async_copy(ref.at[source] if source else ref, to.at[dest] if dest else to, sem.at[i]) for i, (source, dest) in enumerate(moves)]
                  for (_, _, moves), ref, to, sem in zip(weights, weight_refs, held, sems)]

        def ready(which):
            @pl.when(step == 0)
            def _():
                for copy in copies[which]:
                    copy.wait()

        if n_weight:
            @pl.when(step == 0)
            def _():
                for copy in sum(copies, []):
                    copy.start()

        if placing is not None:
            before, after = placing.hooks(steps, step, scalar_refs[0], piece_refs, target[0], *take(3))
            before()
        if n_hand:
            hand_sem, = take(1)
            hands = [pltpu.make_async_copy(ref, to, hand_sem.at[i]) for i, (ref, to) in enumerate(zip(held, handed))]

            @pl.when(step == 1)
            def _():
                for copy in hands:
                    copy.start()

        body(*([ready] if n_weight else []), *scalar_refs, *stream_refs, *const_refs, *held, *out_refs, *refs)
        if placing is not None:
            after()
        if n_hand:
            @pl.when(step == steps - 1)
            def _():
                for copy in hands:
                    copy.wait()

    return pl.pallas_call(
        kernel,
        grid_spec=pltpu.PrefetchScalarGridSpec(num_scalar_prefetch=n_scalar, grid=grid, in_specs=in_specs, out_specs=out_specs, scratch_shapes=scratches),
        out_shape=out_shape, input_output_aliases=aliases,
        compiler_params=pltpu.CompilerParams(dimension_semantics=("arbitrary",) * len(grid), vmem_limit_bytes=VMEM_LIMIT),
        cost_estimate=pl.CostEstimate(flops=flops, bytes_accessed=n_bytes, transcendentals=0))(*scalars, *operands)


def uninitialized(shape, dtype):
    return pl.pallas_call(lambda out: None, out_specs=pl.BlockSpec(memory_space=pl.ANY),
                          out_shape=jax.ShapeDtypeStruct(shape, dtype), name="uninitialized")()


def send_around(block):
    across = lax.ppermute(block, 'x', SWAP)
    beside = lax.ppermute(block, 'core', SWAP)
    diagonal = lax.ppermute(across, 'core', SWAP)
    return [block, beside, across, diagonal]


def block_moves(tp_dim, tp_size, fsdp_dim, fsdp_size):
    moves = []
    for t in range(TP):
        for f in range(FSDP):
            dest = [None, None]
            dest[tp_dim] = pl.ds(t * tp_size, tp_size)
            dest[fsdp_dim] = pl.ds(f * fsdp_size, fsdp_size)
            moves.append(((t * FSDP + f,), tuple(dest)))
    return moves


def device_layer(x_in, seq_lens, grad_out, *weight_shards):
    p = dict(zip(PARAM_NAMES, weight_shards))
    n_seq = x_in.shape[0]
    rows_all = n_seq * L
    tp_index = (lax.axis_index('x') * 2 + lax.axis_index('core')).astype(jnp.int32)
    x_rows = x_in.reshape(rows_all, D)
    dy_rows = grad_out.reshape(rows_all, D)
    rows_mine = rows_all // TP
    rows_chunk = rows_mine // CHUNKS
    rows_part = rows_all // CHUNKS
    seqs_chunk = rows_chunk // L

    vec_names = FSDP_VECTORS + BOTH_VECTORS
    gather = functools.partial(lax.all_gather, axis_name=BOTH, axis=0, tiled=False)
    vec_all = gather(jnp.concatenate([p[name] for name in vec_names])).reshape(TP, FSDP, -1)
    vec, place = {}, 0
    for name in vec_names:
        size = p[name].shape[0]
        part = vec_all[:, :, place:place + size]
        vec[name] = (part[0] if name in FSDP_VECTORS else part).reshape(1, -1).astype(F32)
        place += size
    qkv_blocks = gather(jnp.stack([p[name].reshape(D // 2, D // 4) for name in ('w_query', 'w_key', 'w_value')]))
    qkv_moves = [((owner[0], part), (dest[0], pl.ds(part * D + dest[1].start, D // 4)))
                 for owner, dest in block_moves(1, D // 4, 0, D // 2) for part in range(3)]
    w_qkv = qkv_blocks, (D, 3 * D), qkv_moves
    w_out = gather(p['w_out'].reshape(D // 4, D // 2)), (D, D), block_moves(0, D // 4, 1, D // 2)
    w_fc1 = gather(p['w_fc1']), (D, FF), block_moves(1, FF // 4, 0, D // 2)
    w_fc2 = gather(p['w_fc2']), (FF, D), block_moves(0, FF // 4, 1, D // 2)
    b_qkv = jnp.concatenate([vec['b_query'], vec['b_key'], vec['b_value']], axis=1)
    cos, sin, cos_t, sin_t = rope_tables()

    y_full = uninitialized((rows_all, D), BF16)
    dx_full = uninitialized((rows_all, D), BF16)

    def shared(i, meta, *_):
        return meta[0] + i, 0

    def local(i, *_):
        return i, 0

    def kept(i, meta, *_):
        return meta[2] + i, 0

    def seq3(i, *_):
        return i, 0, 0

    def keep(width):
        return (rows_mine, width), BF16, (L, width), kept

    def pass_on(width, dtype=BF16):
        return (rows_chunk, width), dtype, (L, width), local

    def total(*shape):
        return shape, F32, shape, lambda i, *_: (0,) * len(shape)

    prior_m = {3: uninitialized((rows_mine, D), BF16), 4: uninitialized((rows_mine, FF), BF16), 5: uninitialized((rows_mine, FF), BF16), 6: uninitialized((rows_mine, D), BF16)}
    prior_b = {1: uninitialized((rows_mine, 3 * D), BF16)}
    grid = (seqs_chunk,)
    mlp, bwd = [None] * CHUNKS, [None] * CHUNKS
    y_pieces, dx_pieces = [None] * CHUNKS, [None] * CHUNKS
    x_stream = (x_rows, (L, D), shared)

    def meta_of(c, placing=None, core=0):
        return jnp.stack([jnp.asarray(value, jnp.int32) for value in (
            c * (n_seq // CHUNKS) + tp_index * seqs_chunk, tp_index, c * seqs_chunk, placing.chunk if placing else 0, core)])

    def spread(i, meta, *_):
        return i // seqs_chunk * (n_seq // CHUNKS) + meta[0] + i % seqs_chunk

    whole_move = [(None, None)]
    h1, q, k, v, ctx, stats, w_qkv = call(
        functools.partial(attn_fwd_body, spread), (rows_mine // L,), [meta_of(0), seq_lens],
        [(x_rows, (L, D), lambda i, meta, *_: (spread(i, meta), 0))],
        [b_qkv, vec['ln1_gain'], vec['ln1_bias'], cos, sin], [w_qkv],
        [((rows_mine, D), BF16, (L, D), local)] * 5 + [((rows_mine // L, 2 * HEADS, L), F32, (1, 2 * HEADS, L), seq3)], {}, [],
        rows_mine * (6 * D * D + 64 * L * D), rows_mine * D * 12 + 6 * D * D, hand_on=True)

    arranged = []
    sums_m = [jnp.zeros(shape, F32) for shape in ((4, 8, D), (8, FF))]
    sums_b = [jnp.zeros(shape, F32) for shape in ((2, 8, D), (D, LANES), (2, 8, D))]

    def run_mlp(c, placing=None):
        out = call(
            mlp_body, grid, [meta_of(c, placing)],
            [x_stream, (ctx, (L, D), kept), (dy_rows, (L, D), shared)],
            [vec['b_out'], vec['ln2_gain'], vec['ln2_bias'], vec['b_fc1'], vec['b_fc2']] + sums_m, arranged or [w_out, w_fc1, w_fc2],
            [pass_on(D), pass_on(D, F32), pass_on(D), keep(D), keep(FF), keep(FF), keep(D), total(4, 8, D), total(8, FF)],
            prior_m, [], rows_chunk * (4 * D * D + 16 * D * FF), rows_chunk * (D * 20 + FF * 4) + 18 * D * D, placing, hand_on=not arranged)
        if not arranged:
            arranged.extend((array, array.shape, whole_move) for array in out[9:])
        prior_m.update({i: out[i] for i in prior_m})
        mlp[c] = out
        sums_m[:] = out[7:9]
        y_pieces[c] = send_around(out[0])
        return out[9:] if placing else ()

    def run_bwd(c, placing=None):
        saved = [(array, (L, D), kept) for array in (q, k, v)] + [(mlp[c][2], (L, D), local)]
        out = call(
            attn_bwd_body, grid, [meta_of(c, placing), seq_lens],
            [x_stream] + saved + [(stats, (1, 2 * HEADS, L), lambda i, meta, *_: (meta[2] + i, 0, 0)), (mlp[c][1], (L, D), local)],
            [vec['ln1_gain'], cos, sin, cos_t, sin_t] + sums_b, [(w_qkv, w_qkv.shape, whole_move)],
            [pass_on(D), keep(3 * D), total(2, 8, D), total(D, LANES), total(2, 8, D)], prior_b,
            [pltpu.VMEM((D, L), BF16), pltpu.VMEM((D, L), BF16)],
            rows_chunk * (6 * D * D + 160 * L * D), rows_chunk * D * 22 + 6 * D * D, placing)
        prior_b.update({1: out[1]})
        bwd[c] = out
        sums_b[:] = out[2:5]
        dx_pieces[c] = send_around(out[0])
        return out[5:]

    def weight_grad(lhs, rhs, lhs_index, rhs_index, n_out, size, block, out_index, store, placing=None):
        return call(
            functools.partial(weight_grad_body, store), (n_out, rows_mine // rows_chunk), [meta_of(0, placing)],
            [(lhs, (rows_chunk, D), lhs_index), (rhs, (rows_chunk, D), rhs_index)], [], [],
            [((2, FSDP, 2) + size, F32, block, out_index)], {}, [],
            2 * n_out * rows_mine * D * D, n_out * rows_mine * D * 4, placing)

    def swap_halves_along(axis, halves):
        index = lax.axis_index(axis)
        theirs = lax.ppermute(lax.dynamic_index_in_dim(halves, 1 - index, keepdims=False), axis, SWAP)
        return lax.dynamic_index_in_dim(halves, index, keepdims=False) + theirs

    def scatter(grad):
        size = grad.shape[3:]
        pair = lax.psum_scatter(grad.reshape(-1, size[-1]), ('core', 'fsdp'), scatter_dimension=0, tiled=True).reshape((2,) + size)
        return swap_halves_along('x', pair)

    def by_row(n, k, *_):
        return k, 0

    def by_row_and_part(n, k, *_):
        return k, n

    def by_chunk(n, k, meta):
        return k * TP + meta[1], 0

    half, quarter = D // 2, D // 4
    owners = [(t, f) for t in range(TP) for f in range(FSDP)]

    def store_fc2(acc):
        return [((0, f, 0), acc[:, f * half:(f + 1) * half]) for f in range(FSDP)]

    def store_fc1(acc):
        return [((0, f, 0), acc[f * half:(f + 1) * half]) for f in range(FSDP)]

    def store_qkv(acc):
        return [((t % 2, f, t // 2, 0), acc[f * half:(f + 1) * half, t * quarter:(t + 1) * quarter]) for t, f in owners]

    def store_out(acc):
        return [((t % 2, f, t // 2), acc[t * quarter:(t + 1) * quarter, f * half:(f + 1) * half]) for t, f in owners]

    def store_v(acc):
        return [((t // 2, t % 2, f), acc[f * half:(f + 1) * half, t * quarter:(t + 1) * quarter]) for t, f in owners]

    def owner_block(n, k, *_):
        return n % 2, 0, n // 2, 0, 0

    grads = {}
    last = CHUNKS - 1
    run_mlp(0)
    run_bwd(0)
    run_mlp(1)
    run_bwd(1)
    y_full, = run_mlp(2, Placing(y_pieces[0], y_full, 0))
    dx_full, = run_mlp(3, Placing(dx_pieces[0], dx_full, 0))
    h2, act, du, da_b = mlp[last][3:7]
    grads['w_fc1'] = scatter(weight_grad(h2, du, by_row, by_row_and_part, TP, (half, FF // 4), (1, FSDP, 1, half, FF // 4), owner_block, store_fc1)[0])
    y_full, = run_bwd(2, Placing(y_pieces[1], y_full, 1))
    grad, dx_full = weight_grad(act, dy_rows, by_row_and_part, by_chunk, TP, (FF // 4, half), (1, FSDP, 1, FF // 4, half), owner_block, store_fc2,
                                Placing(dx_pieces[1], dx_full, 1))
    grads['w_fc2'] = scatter(grad)
    y_full, = run_bwd(3, Placing(y_pieces[2], y_full, 2))
    dqkv = bwd[last][1]
    grad, y_full = weight_grad(h1, dqkv, by_row, by_row_and_part, 2, (2, half, quarter), (2, FSDP, 2, 1, half, quarter),
                               lambda n, k, *_: (0, 0, 0, n, 0, 0), store_qkv, Placing(y_pieces[last], y_full, last))
    qk_grad = scatter(grad)
    grad, dx_full = weight_grad(ctx, da_b, by_row, by_row, 1, (quarter, half), (2, FSDP, 2, quarter, half), lambda n, k, *_: (0,) * 5, store_out,
                                Placing(dx_pieces[2], dx_full, 2))
    for axis in ('core', 'fsdp', 'x'):
        grad = swap_halves_along(axis, grad)
    grads['w_out'] = grad.reshape(p['w_out'].shape)
    grad, = weight_grad(h1, dqkv, by_row, lambda n, k, *_: (k, 2), 1, (half, quarter), (2, FSDP, 2, half, quarter), lambda n, k, *_: (0,) * 5, store_v)
    v_grad = lax.psum_scatter(grad.reshape(TP * FSDP, half, quarter), BOTH, scatter_dimension=0, tiled=False)
    for name, grad in zip(('w_query', 'w_key', 'w_value'), (qk_grad[0], qk_grad[1], v_grad)):
        grads[name] = grad.reshape(p[name].shape)
    placing = Placing(dx_pieces[last], dx_full, last)
    dx_full, = call(lambda meta: None, (8,), [meta_of(0, placing)], [], [], [], [], {}, [], 10 ** 9, rows_part * D * 4, placing)

    rows_b, q_sums, kv_sums = sums_b
    rows = jnp.concatenate([rows_b, sums_m[0], kv_sums]).sum(axis=1)
    flat = jnp.concatenate([rows.reshape(-1), q_sums.sum(axis=1), sums_m[1].sum(axis=0)])
    for axis in ('core', 'fsdp', 'x'):
        flat = flat + lax.ppermute(flat, axis, SWAP)
    n_rows = len(FSDP_VECTORS)
    fsdp_index = lax.axis_index('fsdp')
    owner = tp_index * FSDP + fsdp_index
    by_fsdp = lax.dynamic_index_in_dim(flat[:n_rows * D].reshape(n_rows, FSDP, -1), fsdp_index, axis=1, keepdims=False)
    by_owner = lax.dynamic_index_in_dim(flat[n_rows * D:(n_rows + 3) * D].reshape(3, TP * FSDP, -1), owner, axis=1, keepdims=False)
    by_owner_ff = lax.dynamic_index_in_dim(flat[(n_rows + 3) * D:].reshape(TP * FSDP, -1), owner, keepdims=False)
    for name, grad in zip(('ln1_gain', 'ln1_bias', 'ln2_gain', 'ln2_bias', 'b_out', 'b_fc2'), by_fsdp):
        grads[name] = grad
    grads.update(b_key=by_owner[0], b_value=by_owner[1], b_query=by_owner[2], b_fc1=by_owner_ff)
    return (y_full.reshape(x_in.shape), dx_full.reshape(x_in.shape)) + tuple(grads[name] for name in PARAM_NAMES)


def solution(mesh):
    split = jax.sharding.Mesh(mesh.devices.reshape(FSDP, 2, 2), ('fsdp', 'x', 'core'))
    act_spec = P('fsdp', None, None)
    weight_specs = tuple(PARAM_SPECS.values())
    return jax.shard_map(device_layer, mesh=split, in_specs=(act_spec, ROWS, act_spec) + weight_specs,
                         out_specs=(act_spec, act_spec) + weight_specs, check_vma=False)
```

profile of v0, /device:TPU:0, one launch (start us, length us, event | category | flops | bytes accessed | tf_op | source)
XLA Modules:
  0.0 1832.6 jit_solution(7856529895755377505)
XLA Ops:
  53.8 144.1 %shard_map.322 = (bf16[8192,1024]{1,0:T(8,128)(2,1)}, bf16[8192,1024]{1,0:T(8,128)(2,1)}, bf16[8192,1024]{1,0:T(8,128)(2,1)}, bf16[8192,1024]{1,0:T(8,128)(2,1)}...) custom-call(s32[5]{0:T(128)} %get-tuple-element.197.refs_0_, s32[128]{0:T(128)} %refs_1_.9, ...), custom_call_target="tpu_custom_call" | custom-call | flops 188978561024 | bytes 106954752 | tf_op jit(solution)/shard_map/pallas_call | solution.py:411
  199.4 111.4 %shard_map.323 = (bf16[2048,1024]{1,0:T(8,128)(2,1)}, f32[2048,1024]{1,0:T(8,128)}, bf16[2048,1024]{1,0:T(8,128)(2,1)}, bf16[8192,1024]{1,0:T(8,128)(2,1)}, bf16...) custom-call(s32[5]{0:T(128)} %get-tuple-element.197.refs_0_, ...), custom_call_target="tpu_custom_call", output_to_operand_aliasing={{3}: (14, {}), {4}: (15, {}), {5}: (16, {}), {6}: (17, {})} | custom-call | flops 146028888064 | bytes 94371840 | tf_op jit(solution)/shard_map/pallas_call | solution.py:411
  313.7 53.8 %shard_map.326 = (bf16[2048,1024]{1,0:T(8,128)(2,1)}, bf16[8192,3072]{1,0:T(8,128)(2,1)}, f32[2,8,1024]{2,1,0:T(8,128)}, f32[1024,128]{1,0:T(8,128)}, f32[2,8,1024]{2,1,0:T(8,128)}) custom-call(s32[5]{0:T(128)} %get-tuple-element.197.refs_0_, s32[128]{0:T(128)} %refs_1_.9, ...), custom_call_target="tpu_custom_call", output_to_operand_aliasing={{1}: (18, {})} | custom-call | flops 98784247808 | bytes 52428800 | tf_op jit(solution)/shard_map/pallas_call | solution.py:411
  368.3 36.2 %collective-permute-done.1.refs_20_ = bf16[2048,1024]{1,0:T(8,128)(2,1)} collective-permute-done((bf16[2048,1024]{1,0:T(8,128)(2,1)}, bf16[2048,1024]{1,0:T(8,128)(2,1)}, u32[]{:S(2)}, u32[]{:S(2)}) %collective-permute-start.1) | collective-permute-done | bytes 4194336 | tf_op jit(solution)/shard_map/ppermute | solution.py:425
  404.6 110.0 %shard_map.324 = (bf16[2048,1024]{1,0:T(8,128)(2,1)}, f32[2048,1024]{1,0:T(8,128)}, bf16[2048,1024]{1,0:T(8,128)(2,1)}, bf16[8192,1024]{1,0:T(8,128)(2,1)}, bf16...) custom-call(s32[5]{0:T(128)} %get-tuple-element.194.refs_0_, ...), custom_call_target="tpu_custom_call", output_to_operand_aliasing={{3}: (14, {}), {4}: (15, {}), {5}: (16, {}), {6}: (17, {})} | custom-call | flops 146028888064 | bytes 94371840 | tf_op jit(solution)/shard_map/pallas_call | solution.py:411
  515.1 112.7 %shard_map.325 = (bf16[2048,1024]{1,0:T(8,128)(2,1)}, f32[2048,1024]{1,0:T(8,128)}, bf16[2048,1024]{1,0:T(8,128)(2,1)}, bf16[8192,1024]{1,0:T(8,128)(2,1)}, bf16...) custom-call(s32[5]{0:T(128)} %get-tuple-element.196.refs_0_, ...), custom_call_target="tpu_custom_call", output_to_operand_aliasing={{3}: (14, {}), {4}: (15, {}), {5}: (16, {}), {6}: (17, {}),... | custom-call | flops 146028888064 | bytes 94371840 | tf_op jit(solution)/shard_map/pallas_call | solution.py:411
  627.9 113.0 %shard_map.327 = (bf16[2048,1024]{1,0:T(8,128)(2,1)}, f32[2048,1024]{1,0:T(8,128)}, bf16[2048,1024]{1,0:T(8,128)(2,1)}, bf16[8192,1024]{1,0:T(8,128)(2,1)}, bf16...) custom-call(s32[5]{0:T(128)} %get-tuple-element.195.refs_0_, ...), custom_call_target="tpu_custom_call", output_to_operand_aliasing={{3}: (14, {}), {4}: (15, {}), {5}: (16, {}), {6}: (17, {}),... | custom-call | flops 146028888064 | bytes 94371840 | tf_op jit(solution)/shard_map/pallas_call | solution.py:411
  740.9 85.7 %shard_map.336 = f32[2,2,2,512,1024]{4,3,2,1,0:T(8,128)} custom-call(s32[5]{0:T(128)} %get-tuple-element.197.refs_0_, bf16[8192,1024]{1,0:T(8,128)(2,1)} %get-tuple-element.167.refs_1_, bf16[8192,4096]{1,0:T(8,128)(2,1)} %get-tuple-element.168.refs_2_), custom_call_target="tpu_custom_call" | custom-call | flops 68719476736 | bytes 134217728 | tf_op jit(solution)/shard_map/pallas_call | solution.py:411
  826.6 53.8 %shard_map.328 = (bf16[2048,1024]{1,0:T(8,128)(2,1)}, bf16[8192,3072]{1,0:T(8,128)(2,1)}, f32[2,8,1024]{2,1,0:T(8,128)}, f32[1024,128]{1,0:T(8,128)}, f32[2,8,1024]{2,1,0:T(8,128)}) custom-call(s32[5]{0:T(128)} %get-tuple-element.194.refs_0_, s32[128]{0:T(128)} %refs_1_.9, ...), custom_call_target="tpu_custom_call", output_to_operand_aliasing={{1}: (18, {})} | custom-call | flops 98784247808 | bytes 52428800 | tf_op jit(solution)/shard_map/pallas_call | solution.py:411
  881.4 91.6 %collective-permute-done.22.refs_5_ = bf16[2048,1024]{1,0:T(8,128)(2,1)} collective-permute-done((bf16[2048,1024]{1,0:T(8,128)(2,1)}, bf16[2048,1024]{1,0:T(8,128)(2,1)}, u32[]{:S(2)}, u32[]{:S(2)}) %collective-permute-start.22) | collective-permute-done | bytes 4194336 | tf_op jit(solution)/shard_map/ppermute | solution.py:425
  980.4 91.7 %shard_map.332 = (f32[2,2,2,1024,512]{4,3,2,1,0:T(8,128)}, bf16[32768,1024]{1,0:T(8,128)(2,1)}) custom-call(s32[5]{0:T(128)} %stack.44.refs_0_, bf16[8192,4096]{1,0:T(8,128)(2,1)} %get-tuple-element.155.refs_1_, bf16[32768,1024]{1,0:T(8,128)(2,1)} %bitcast.8.refs_3_.refs_2_, ...), custom_call_target="tpu_custom_call", output_to_operand_aliasing={{1}: (7, {})} | custom-call | flops 68719476736 | bytes 134217728 | tf_op jit(solution)/shard_map/pallas_call | solution.py:411
  1074.3 91.7 %collective-permute-done.7.refs_21_ = bf16[2048,1024]{1,0:T(8,128)(2,1)} collective-permute-done((bf16[2048,1024]{1,0:T(8,128)(2,1)}, bf16[2048,1024]{1,0:T(8,128)(2,1)}, u32[]{:S(2)}, u32[]{:S(2)}) %collective-permute-start.7) | collective-permute-done | bytes 4194336 | tf_op jit(solution)/shard_map/ppermute | solution.py:425
  1169.6 86.3 %collective-permute-done.10.refs_21_ = bf16[2048,1024]{1,0:T(8,128)(2,1)} collective-permute-done((bf16[2048,1024]{1,0:T(8,128)(2,1)}, bf16[2048,1024]{1,0:T(8,128)(2,1)}, u32[]{:S(2)}, u32[]{:S(2)}) %collective-permute-start.10) | collective-permute-done | bytes 4194336 | tf_op jit(solution)/shard_map/ppermute | solution.py:425
  1255.9 55.5 %shard_map.329 = (bf16[2048,1024]{1,0:T(8,128)(2,1)}, bf16[8192,3072]{1,0:T(8,128)(2,1)}, f32[2,8,1024]{2,1,0:T(8,128)}, f32[1024,128]{1,0:T(8,128)}, f32[2,8,10...) custom-call(s32[5]{0:T(128)} %stack.42.refs_0_, s32[128]{0:T(128)} %refs_1_.9, ...), custom_call_target="tpu_custom_call", output_to_operand_aliasing={{1}: (18, {}), {5}: (23, {})} | custom-call | flops 98784247808 | bytes 52428800 | tf_op jit(solution)/shard_map/pallas_call | solution.py:411
  1311.5 33.5 %collective-permute-done.13.refs_5_ = bf16[2048,1024]{1,0:T(8,128)(2,1)} collective-permute-done((bf16[2048,1024]{1,0:T(8,128)(2,1)}, bf16[2048,1024]{1,0:T(8,128)(2,1)}, u32[]{:S(2)}, u32[]{:S(2)}) %collective-permute-start.13) | collective-permute-done | bytes 4194336 | tf_op jit(solution)/shard_map/ppermute | solution.py:425
  1345.0 55.8 %shard_map.330 = (bf16[2048,1024]{1,0:T(8,128)(2,1)}, bf16[8192,3072]{1,0:T(8,128)(2,1)}, f32[2,8,1024]{2,1,0:T(8,128)}, f32[1024,128]{1,0:T(8,128)}, f32[2,8,10...) custom-call(s32[5]{0:T(128)} %stack.36.refs_0_, s32[128]{0:T(128)} %refs_1_.9, ...), custom_call_target="tpu_custom_call", output_to_operand_aliasing={{1}: (18, {}), {5}: (23, {})} | custom-call | flops 98784247808 | bytes 52428800 | tf_op jit(solution)/shard_map/pallas_call | solution.py:411
  1400.8 52.1 %shard_map.331 = (f32[2,2,2,2,512,256]{5,4,3,2,1,0:T(8,128)}, bf16[32768,1024]{1,0:T(8,128)(2,1)}) custom-call(s32[5]{0:T(128)} %stack.32.refs_0_, bf16[8192,1024]{1,0:T(8,128)(2,1)} %get-tuple-element.94.refs_1_, bf16[8192,3072]{1,0:T(8,128)(2,1)} %get-tuple-element.148.refs_2_, ...), custom_call_target="tpu_custom_call", output_to_operand_aliasing={{1}: (7, {})} | custom-call | flops 34359738368 | bytes 67108864 | tf_op jit(solution)/shard_map/pallas_call | solution.py:411
  1454.4 91.8 %collective-permute-done.19.refs_5_ = bf16[2048,1024]{1,0:T(8,128)(2,1)} collective-permute-done((bf16[2048,1024]{1,0:T(8,128)(2,1)}, bf16[2048,1024]{1,0:T(8,128)(2,1)}, u32[]{:S(2)}, u32[]{:S(2)}) %collective-permute-start.19) | collective-permute-done | bytes 4194336 | tf_op jit(solution)/shard_map/ppermute | solution.py:425
  1548.1 26.1 %shard_map.335 = f32[2,2,2,512,256]{4,3,2,1,0:T(8,128)} custom-call(s32[5]{0:T(128)} %get-tuple-element.197.refs_0_, bf16[8192,1024]{1,0:T(8,128)(2,1)} %get-tuple-element.94.refs_1_, bf16[8192,3072]{1,0:T(8,128)(2,1)} %get-tuple-element.148.refs_2_), custom_call_target="tpu_custom_call" | custom-call | flops 17179869184 | bytes 33554432 | tf_op jit(solution)/shard_map/pallas_call | solution.py:411
  1574.2 34.7 %shard_map.333 = (f32[2,2,2,256,512]{4,3,2,1,0:T(8,128)}, bf16[32768,1024]{1,0:T(8,128)(2,1)}) custom-call(s32[5]{0:T(128)} %stack.43.refs_0_, bf16[8192,1024]{1,0:T(8,128)(2,1)} %get-tuple-element.98.refs_2_.refs_1_, bf16[8192,1024]{1,0:T(8,128)(2,1)} %get-tuple-element.153.refs_2_, ...), custom_call_target="tpu_custom_call", output_to_operand_aliasing={{1}: (7, {})} | custom-call | flops 17179869184 | bytes 33554432 | tf_op jit(solution)/shard_map/pallas_call | solution.py:411
  1611.4 45.5 %collective-permute-done.16.refs_3_ = bf16[2048,1024]{1,0:T(8,128)(2,1)} collective-permute-done((bf16[2048,1024]{1,0:T(8,128)(2,1)}, bf16[2048,1024]{1,0:T(8,128)(2,1)}, u32[]{:S(2)}, u32[]{:S(2)}) %collective-permute-start.16) | collective-permute-done | bytes 4194336 | tf_op jit(solution)/shard_map/ppermute | solution.py:425
  1663.1 22.4 %collective-permute-done.29 = f32[2,256,512]{2,1,0:T(8,128)} collective-permute-done((f32[2,256,512]{2,1,0:T(8,128)S(1)}, f32[2,256,512]{2,1,0:T(8,128)}, u32[]{:S(2)}, u32[]{:S(2)}) %collective-permute-start.29) | collective-permute-done | bytes 1048608 | tf_op jit(solution)/shard_map/ppermute | solution.py:562
  1700.7 45.8 %collective-permute-done.26 = f32[13312]{0:T(1024)S(1)} collective-permute-done((f32[13312]{0:T(1024)S(1)}, f32[13312]{0:T(1024)S(1)}, u32[]{:S(2)}, u32[]{:S(2)}) %collective-permute-start.26) | collective-permute-done | bytes 53280 | tf_op jit(solution)/shard_map/ppermute | solution.py:635
  1774.5 41.3 %collective-permute-done.27 = f32[2,512,256]{1,2,0:T(8,128)} collective-permute-done((f32[2,512,256]{1,2,0:T(8,128)}, f32[2,512,256]{1,2,0:T(8,128)}, u32[]{:S(2)}, u32[]{:S(2)}) %collective-permute-start.27) | collective-permute-done | bytes 1048608 | tf_op jit(solution)/shard_map/ppermute | solution.py:562
  (197 shorter events, 131.1 us)
Async XLA Ops:
  9.7 188.3 %all-gather.10.cloned.1.call-start = ((), (), s32[]{:S(2)}) async-start(), calls=%async_computation.4 | async-start | bytes 2359296 | tf_op jit(solution)/shard_map/all_gather | solution.py:467
  10.5 187.5 %all-gather.14.cloned.1.call-start = ((), (), s32[]{:S(2)}) async-start(), calls=%async_computation.10 | async-start | bytes 9437184 | tf_op jit(solution)/shard_map/all_gather | solution.py:468
  11.2 186.8 %all-gather.16.cloned.1.call-start = ((), (), s32[]{:S(2)}) async-start(), calls=%async_computation.11 | async-start | bytes 9437184 | tf_op jit(solution)/shard_map/all_gather | solution.py:469
  11.8 1676.5 %reduce-scatter.9.cloned.1.call-start = ((), (), s32[]{:S(2)}) async-start(), calls=%async_computation.7 | async-start | bytes 20971520 | tf_op jit(solution)/shard_map/reduce_scatter | solution.py:567
  310.8 204.4 %collective-permute-start = (bf16[2048,1024]{1,0:T(8,128)(2,1)}, bf16[2048,1024]{1,0:T(8,128)(2,1)}, u32[]{:S(2)}, u32[]{:S(2)}) collective-permute-start(bf16[2048,1024]{1,0:T(8,128)(2,1)} %get-tuple-element.114.refs_18_), channel_id=1, source_target_pairs={{0,1},{1,0},{2,3},{3,2},{4,5},{5,4},{6,7},{7,6}} | collective-permute-start | bytes 12582920 | tf_op jit(solution)/shard_map/ppermute | solution.py:426
  310.8 93.8 %collective-permute-start.1 = (bf16[2048,1024]{1,0:T(8,128)(2,1)}, bf16[2048,1024]{1,0:T(8,128)(2,1)}, u32[]{:S(2)}, u32[]{:S(2)}) collective-permute-start(bf16[2048,1024]{1,0:T(8,128)(2,1)} %get-tuple-element.114.refs_18_), channel_id=1, source_target_pairs={{0,2},{2,0},{1,3},{3,1},{4,6},{6,4},{5,7},{7,5}} | collective-permute-start | bytes 12582920 | tf_op jit(solution)/shard_map/ppermute | solution.py:425
  367.6 260.3 %collective-permute-start.3 = (bf16[2048,1024]{1,0:T(8,128)(2,1)}, bf16[2048,1024]{1,0:T(8,128)(2,1)}, u32[]{:S(2)}, u32[]{:S(2)}) collective-permute-start(bf16[2048,1024]{1,0:T(8,128)(2,1)} %get-tuple-element.125.refs_18_), channel_id=1, source_target_pairs={{0,1},{1,0},{2,3},{3,2},{4,5},{5,4},{6,7},{7,6}} | collective-permute-start | bytes 12582920 | tf_op jit(solution)/shard_map/ppermute | solution.py:426
  367.7 146.8 %collective-permute-start.4 = (bf16[2048,1024]{1,0:T(8,128)(2,1)}, bf16[2048,1024]{1,0:T(8,128)(2,1)}, u32[]{:S(2)}, u32[]{:S(2)}) collective-permute-start(bf16[2048,1024]{1,0:T(8,128)(2,1)} %get-tuple-element.125.refs_18_), channel_id=1, source_target_pairs={{0,2},{2,0},{1,3},{3,1},{4,6},{6,4},{5,7},{7,5}} | collective-permute-start | bytes 12582920 | tf_op jit(solution)/shard_map/ppermute | solution.py:425
  404.6 110.5 %collective-permute-start.2 = (bf16[2048,1024]{1,0:T(8,128)(2,1)}, bf16[2048,1024]{1,0:T(8,128)(2,1)}, u32[]{:S(2)}, u32[]{:S(2)}) collective-permute-start(bf16[2048,1024]{1,0:T(8,128)(2,1)} %collective-permute-done.1.refs_20_), channel_id=1, source_target_pairs={{0,1},{1,0},{2,3},{3,2},{4,5},{5,4},{6,7},{7,6}} | collective-permute-start | bytes 12582920 | tf_op jit(solution)/shard_map/ppermute | solution.py:427
  514.6 113.3 %collective-permute-start.5 = (bf16[2048,1024]{1,0:T(8,128)(2,1)}, bf16[2048,1024]{1,0:T(8,128)(2,1)}, u32[]{:S(2)}, u32[]{:S(2)}) collective-permute-start(bf16[2048,1024]{1,0:T(8,128)(2,1)} %collective-permute-done.4.refs_20_), channel_id=1, source_target_pairs={{0,1},{1,0},{2,3},{3,2},{4,5},{5,4},{6,7},{7,6}} | collective-permute-start | bytes 12582920 | tf_op jit(solution)/shard_map/ppermute | solution.py:427
  826.6 871.1 %reduce-scatter.11.cloned.1.call-start = ((), (), s32[]{:S(2)}) async-start(), calls=%async_computation.8 | async-start | bytes 20971520 | tf_op jit(solution)/shard_map/reduce_scatter | solution.py:567
  1072.2 675.6 %reduce-scatter.5.cloned.1.call-start = ((), (), s32[]{:S(2)}) async-start(), calls=%async_computation.5 | async-start | bytes 10485760 | tf_op jit(solution)/shard_map/reduce_scatter | solution.py:567
  1072.2 93.8 %collective-permute-start.7 = (bf16[2048,1024]{1,0:T(8,128)(2,1)}, bf16[2048,1024]{1,0:T(8,128)(2,1)}, u32[]{:S(2)}, u32[]{:S(2)}) collective-permute-start(bf16[2048,1024]{1,0:T(8,128)(2,1)} %get-tuple-element.140.refs_19_), channel_id=1, source_target_pairs={{0,2},{2,0},{1,3},{3,1},{4,6},{6,4},{5,7},{7,5}} | collective-permute-start | bytes 12582920 | tf_op jit(solution)/shard_map/ppermute | solution.py:425
  1073.5 94.8 %collective-permute-start.6 = (bf16[2048,1024]{1,0:T(8,128)(2,1)}, bf16[2048,1024]{1,0:T(8,128)(2,1)}, u32[]{:S(2)}, u32[]{:S(2)}) collective-permute-start(bf16[2048,1024]{1,0:T(8,128)(2,1)} %get-tuple-element.140.refs_19_), channel_id=1, source_target_pairs={{0,1},{1,0},{2,3},{3,2},{4,5},{5,4},{6,7},{7,6}} | collective-permute-start | bytes 12582920 | tf_op jit(solution)/shard_map/ppermute | solution.py:426
  1073.5 182.4 %collective-permute-start.10 = (bf16[2048,1024]{1,0:T(8,128)(2,1)}, bf16[2048,1024]{1,0:T(8,128)(2,1)}, u32[]{:S(2)}, u32[]{:S(2)}) collective-permute-start(bf16[2048,1024]{1,0:T(8,128)(2,1)} %get-tuple-element.146.refs_19_), channel_id=1, source_target_pairs={{0,2},{2,0},{1,3},{3,1},{4,6},{6,4},{5,7},{7,5}} | collective-permute-start | bytes 12582920 | tf_op jit(solution)/shard_map/ppermute | solution.py:425
  1167.8 177.1 %collective-permute-start.9 = (bf16[2048,1024]{1,0:T(8,128)(2,1)}, bf16[2048,1024]{1,0:T(8,128)(2,1)}, u32[]{:S(2)}, u32[]{:S(2)}) collective-permute-start(bf16[2048,1024]{1,0:T(8,128)(2,1)} %get-tuple-element.146.refs_19_), channel_id=1, source_target_pairs={{0,1},{1,0},{2,3},{3,2},{4,5},{5,4},{6,7},{7,6}} | collective-permute-start | bytes 12582920 | tf_op jit(solution)/shard_map/ppermute | solution.py:426
  1168.3 232.4 %collective-permute-start.12 = (bf16[2048,1024]{1,0:T(8,128)(2,1)}, bf16[2048,1024]{1,0:T(8,128)(2,1)}, u32[]{:S(2)}, u32[]{:S(2)}) collective-permute-start(bf16[2048,1024]{1,0:T(8,128)(2,1)} %get-tuple-element.149.refs_3_), channel_id=1, source_target_pairs={{0,1},{1,0},{2,3},{3,2},{4,5},{5,4},{6,7},{7,6}} | collective-permute-start | bytes 12582920 | tf_op jit(solution)/shard_map/ppermute | solution.py:426
  1168.3 176.6 %collective-permute-start.13 = (bf16[2048,1024]{1,0:T(8,128)(2,1)}, bf16[2048,1024]{1,0:T(8,128)(2,1)}, u32[]{:S(2)}, u32[]{:S(2)}) collective-permute-start(bf16[2048,1024]{1,0:T(8,128)(2,1)} %get-tuple-element.149.refs_3_), channel_id=1, source_target_pairs={{0,2},{2,0},{1,3},{3,1},{4,6},{6,4},{5,7},{7,5}} | collective-permute-start | bytes 12582920 | tf_op jit(solution)/shard_map/ppermute | solution.py:425
  1452.9 302.4 %reduce-scatter.7.cloned.1.call-start = ((), (), s32[]{:S(2)}) async-start(), calls=%async_computation.6 | async-start | bytes 4718592 | tf_op jit(solution)/shard_map/reduce_scatter | solution.py:625
  1454.2 119.9 %collective-permute-start.18 = (bf16[2048,1024]{1,0:T(8,128)(2,1)}, bf16[2048,1024]{1,0:T(8,128)(2,1)}, u32[]{:S(2)}, u32[]{:S(2)}) collective-permute-start(bf16[2048,1024]{1,0:T(8,128)(2,1)} %get-tuple-element.154.refs_3_), channel_id=1, source_target_pairs={{0,1},{1,0},{2,3},{3,2},{4,5},{5,4},{6,7},{7,6}} | collective-permute-start | bytes 12582920 | tf_op jit(solution)/shard_map/ppermute | solution.py:426
  1546.8 110.2 %collective-permute-start.16 = (bf16[2048,1024]{1,0:T(8,128)(2,1)}, bf16[2048,1024]{1,0:T(8,128)(2,1)}, u32[]{:S(2)}, u32[]{:S(2)}) collective-permute-start(bf16[2048,1024]{1,0:T(8,128)(2,1)} %get-tuple-element.152.refs_1_), channel_id=1, source_target_pairs={{0,2},{2,0},{1,3},{3,1},{4,6},{6,4},{5,7},{7,5}} | collective-permute-start | bytes 12582920 | tf_op jit(solution)/shard_map/ppermute | solution.py:425
  1611.4 146.0 %collective-permute-start.15 = (bf16[2048,1024]{1,0:T(8,128)(2,1)}, bf16[2048,1024]{1,0:T(8,128)(2,1)}, u32[]{:S(2)}, u32[]{:S(2)}) collective-permute-start(bf16[2048,1024]{1,0:T(8,128)(2,1)} %get-tuple-element.152.refs_1_), channel_id=1, source_target_pairs={{0,1},{1,0},{2,3},{3,2},{4,5},{5,4},{6,7},{7,6}} | collective-permute-start | bytes 12582920 | tf_op jit(solution)/shard_map/ppermute | solution.py:426
  1656.9 100.4 %collective-permute-start.17 = (bf16[2048,1024]{1,0:T(8,128)(2,1)}, bf16[2048,1024]{1,0:T(8,128)(2,1)}, u32[]{:S(2)}, u32[]{:S(2)}) collective-permute-start(bf16[2048,1024]{1,0:T(8,128)(2,1)} %collective-permute-done.16.refs_3_), channel_id=1, source_target_pairs={{0,1},{1,0},{2,3},{3,2},{4,5},{5,4},{6,7},{7,6}} | collective-permute-start | bytes 12582920 | tf_op jit(solution)/shard_map/ppermute | solution.py:427
  1691.4 126.8 %collective-permute-start.31 = (f32[512,1024]{1,0:T(8,128)}, f32[512,1024]{1,0:T(8,128)}, u32[]{:S(2)}, u32[]{:S(2)}) collective-permute-start(f32[512,1024]{1,0:T(8,128)} %dynamic-slice_bitcast_fusion.1), channel_id=1, source_target_pairs={{0,2},{2,0},{1,3},{3,1},{4,6},{6,4},{5,7},{7,5}} | collective-permute-start | bytes 6291464 | tf_op jit(solution)/shard_map/ppermute | solution.py:562
  (32 other events, 1073.5 us)
Sparse Core Ops, SparseCore 0:
  10.5 43.3 all-gather.11
  55.6 22.2 all-gather.9
  79.7 48.6 all-gather.13
  130.1 48.6 all-gather.15
  826.7 119.6 reduce-scatter.8
  1072.3 121.2 reduce-scatter.10
  1453.0 67.6 reduce-scatter.4
  1574.3 59.3 reduce-scatter.6
where the time goes:
time: 1840 us; the launch traced here: 1830 us
  Pallas kernels  1120 us (61%)
  waiting for transfers between devices  614 us (33%)
  local copies, waits for them, and re-layouts  32 us (2%)
  other arithmetic  21.7 us (1%)
  starting transfers between devices  18.6 us (1%)
    pallas_call x15, Pallas kernels, call(): pl.pallas_call(kernel, grid_spec=pltpu.PrefetchScalarGridSpec(num_scalar_...  1120 us
    ppermute x8, waiting for transfers between devices, send_around(): across = lax.ppermute(block, 'x', SWAP)  477 us
    ppermute x6, waiting for transfers between devices, swap_halves_along(): lax.ppermute(lax.dynamic_index_in_dim(halves, 1 - index, keepdims=False),...  63.7 us
    ppermute x3, waiting for transfers between devices, device_layer(): flat = flat + lax.ppermute(flat, axis, SWAP)  49.2 us
  transfers between devices with their start and end apart: 41, of which 13 were waited for; matrix products, arithmetic and copies ran while one was open for 3% of the time, Pallas kernels for 44%

commit v1 on v0

--- a/solution.py
+++ b/solution.py
@@ -550,10 +550,10 @@
         dx_pieces[c] = send_around(out[0])
         return out[5:]
 
-    def weight_grad(lhs, rhs, lhs_index, rhs_index, n_out, size, block, out_index, store, placing=None):
+    def weight_grad(lhs, rhs, lhs_index, rhs_index, n_out, size, block, out_index, store, placing=None, tile=rows_chunk):
         return call(
-            functools.partial(weight_grad_body, store), (n_out, rows_mine // rows_chunk), [meta_of(0, placing)],
-            [(lhs, (rows_chunk, D), lhs_index), (rhs, (rows_chunk, D), rhs_index)], [], [],
+            functools.partial(weight_grad_body, store), (n_out, rows_mine // tile), [meta_of(0, placing)],
+            [(lhs, (tile, D), lhs_index), (rhs, (tile, D), rhs_index)], [], [],
             [((2, FSDP, 2) + size, F32, block, out_index)], {}, [],
             2 * n_out * rows_mine * D * D, n_out * rows_mine * D * 4, placing)
 
@@ -592,7 +592,7 @@
         return [((t % 2, f, t // 2), acc[t * quarter:(t + 1) * quarter, f * half:(f + 1) * half]) for t, f in owners]
 
     def store_v(acc):
-        return [((t // 2, t % 2, f), acc[f * half:(f + 1) * half, t * quarter:(t + 1) * quarter]) for t, f in owners]
+        return [((t % 2, t // 2, f), acc[f * half:(f + 1) * half, t * quarter:(t + 1) * quarter]) for t, f in owners]
 
     def owner_block(n, k, *_):
         return n % 2, 0, n // 2, 0, 0
@@ -606,7 +606,8 @@
     y_full, = run_mlp(2, Placing(y_pieces[0], y_full, 0))
     dx_full, = run_mlp(3, Placing(dx_pieces[0], dx_full, 0))
     h2, act, du, da_b = mlp[last][3:7]
-    grads['w_fc1'] = scatter(weight_grad(h2, du, by_row, by_row_and_part, TP, (half, FF // 4), (1, FSDP, 1, half, FF // 4), owner_block, store_fc1)[0])
+    grads['w_fc1'] = scatter(weight_grad(h2, du, by_row, by_row_and_part, TP, (half, FF // 4), (1, FSDP, 1, half, FF // 4), owner_block, store_fc1,
+                                               tile=2 * rows_chunk)[0])
     y_full, = run_bwd(2, Placing(y_pieces[1], y_full, 1))
     grad, dx_full = weight_grad(act, dy_rows, by_row_and_part, by_chunk, TP, (FF // 4, half), (1, FSDP, 1, FF // 4, half), owner_block, store_fc2,
                                 Placing(dx_pieces[1], dx_full, 1))
@@ -621,8 +622,10 @@
     for axis in ('core', 'fsdp', 'x'):
         grad = swap_halves_along(axis, grad)
     grads['w_out'] = grad.reshape(p['w_out'].shape)
-    grad, = weight_grad(h1, dqkv, by_row, lambda n, k, *_: (k, 2), 1, (half, quarter), (2, FSDP, 2, half, quarter), lambda n, k, *_: (0,) * 5, store_v)
-    v_grad = lax.psum_scatter(grad.reshape(TP * FSDP, half, quarter), BOTH, scatter_dimension=0, tiled=False)
+    v_grad, = weight_grad(h1, dqkv, by_row, lambda n, k, *_: (k, 2), 1, (half, quarter), (2, FSDP, 2, half, quarter), lambda n, k, *_: (0,) * 5, store_v,
+                          tile=2 * rows_chunk)
+    for axis in ('core', 'x', 'fsdp'):
+        v_grad = swap_halves_along(axis, v_grad)
     for name, grad in zip(('w_query', 'w_key', 'w_value'), (qk_grad[0], qk_grad[1], v_grad)):
         grads[name] = grad.reshape(p[name].shape)
     placing = Placing(dx_pieces[last], dx_full, last)

time: 1840 us -> 1830 us (level)
  waiting for transfers between devices: 614 us -> 595 us
    ppermute x3, waiting for transfers between devices: 49.2 us -> 24.4 us  [device_layer(): flat = flat + lax.ppermute(flat, axis, SWAP)]
    ppermute x6 -> x9, waiting for transfers between devices: 63.7 us -> 88.1 us  [swap_halves_along(): lax.ppermute(lax.dynamic_index_in_dim(halves, 1 - index, keepdims=False),...]
    ppermute x8, waiting for transfers between devices: 477 us -> 458 us  [send_around(): across = lax.ppermute(block, 'x', SWAP)]
  transfers between devices with their start and end apart: 41 -> 43, of which waited for: 13 -> 14; matrix products, arithmetic and copies ran while one was open for 3% -> 3% of each run, Pallas kernels for 44% -> 44%
where the time goes in v1:
time: 1830 us; the launch traced here: 1820 us
  Pallas kernels  1110 us (61%)
  waiting for transfers between devices  595 us (33%)
  local copies, waits for them, and re-layouts  37.9 us (2%)
  other arithmetic  25.6 us (1%)
  starting transfers between devices  21 us (1%)
    pallas_call x15, Pallas kernels, call(): pl.pallas_call(kernel, grid_spec=pltpu.PrefetchScalarGridSpec(num_scalar_...  1110 us
    ppermute x8, waiting for transfers between devices, send_around(): across = lax.ppermute(block, 'x', SWAP)  458 us
    ppermute x9, waiting for transfers between devices, swap_halves_along(): lax.ppermute(lax.dynamic_index_in_dim(halves, 1 - index, keepdims=False),...  88.1 us
  transfers between devices with their start and end apart: 43, of which 14 were waited for; matrix products, arithmetic and copies ran while one was open for 3% of the time, Pallas kernels for 44%

profile of v1, /device:TPU:0, one launch (start us, length us, event | category | flops | bytes accessed | tf_op | source)
XLA Modules:
  0.0 1821.0 jit_solution(12293511370681909290)
XLA Ops:
  37.9 15.9 all-gather.12.cloned.1.call-done
  53.8 143.9 %shard_map.322 = (bf16[8192,1024]{1,0:T(8,128)(2,1)}, bf16[8192,1024]{1,0:T(8,128)(2,1)}, bf16[8192,1024]{1,0:T(8,128)(2,1)}, bf16[8192,1024]{1,0:T(8,128)(2,1)}...) custom-call(s32[5]{0:T(128)} %get-tuple-element.215.refs_0_, s32[128]{0:T(128)} %refs_1_.9, ...), custom_call_target="tpu_custom_call" | custom-call | flops 188978561024 | bytes 106954752 | tf_op jit(solution)/shard_map/pallas_call | solution.py:411
  199.2 111.4 %shard_map.323 = (bf16[2048,1024]{1,0:T(8,128)(2,1)}, f32[2048,1024]{1,0:T(8,128)}, bf16[2048,1024]{1,0:T(8,128)(2,1)}, bf16[8192,1024]{1,0:T(8,128)(2,1)}, bf16...) custom-call(s32[5]{0:T(128)} %get-tuple-element.215.refs_0_, ...), custom_call_target="tpu_custom_call", output_to_operand_aliasing={{3}: (14, {}), {4}: (15, {}), {5}: (16, {}), {6}: (17, {})} | custom-call | flops 146028888064 | bytes 94371840 | tf_op jit(solution)/shard_map/pallas_call | solution.py:411
  313.8 53.8 %shard_map.326 = (bf16[2048,1024]{1,0:T(8,128)(2,1)}, bf16[8192,3072]{1,0:T(8,128)(2,1)}, f32[2,8,1024]{2,1,0:T(8,128)}, f32[1024,128]{1,0:T(8,128)}, f32[2,8,1024]{2,1,0:T(8,128)}) custom-call(s32[5]{0:T(128)} %get-tuple-element.215.refs_0_, s32[128]{0:T(128)} %refs_1_.9, ...), custom_call_target="tpu_custom_call", output_to_operand_aliasing={{1}: (18, {})} | custom-call | flops 98784247808 | bytes 52428800 | tf_op jit(solution)/shard_map/pallas_call | solution.py:411
  368.3 36.3 %collective-permute-done.1.refs_20_ = bf16[2048,1024]{1,0:T(8,128)(2,1)} collective-permute-done((bf16[2048,1024]{1,0:T(8,128)(2,1)}, bf16[2048,1024]{1,0:T(8,128)(2,1)}, u32[]{:S(2)}, u32[]{:S(2)}) %collective-permute-start.1) | collective-permute-done | bytes 4194336 | tf_op jit(solution)/shard_map/ppermute | solution.py:425
  404.6 110.0 %shard_map.324 = (bf16[2048,1024]{1,0:T(8,128)(2,1)}, f32[2048,1024]{1,0:T(8,128)}, bf16[2048,1024]{1,0:T(8,128)(2,1)}, bf16[8192,1024]{1,0:T(8,128)(2,1)}, bf16...) custom-call(s32[5]{0:T(128)} %get-tuple-element.212.refs_0_, ...), custom_call_target="tpu_custom_call", output_to_operand_aliasing={{3}: (14, {}), {4}: (15, {}), {5}: (16, {}), {6}: (17, {})} | custom-call | flops 146028888064 | bytes 94371840 | tf_op jit(solution)/shard_map/pallas_call | solution.py:411
  515.2 112.7 %shard_map.325 = (bf16[2048,1024]{1,0:T(8,128)(2,1)}, f32[2048,1024]{1,0:T(8,128)}, bf16[2048,1024]{1,0:T(8,128)(2,1)}, bf16[8192,1024]{1,0:T(8,128)(2,1)}, bf16...) custom-call(s32[5]{0:T(128)} %get-tuple-element.214.refs_0_, ...), custom_call_target="tpu_custom_call", output_to_operand_aliasing={{3}: (14, {}), {4}: (15, {}), {5}: (16, {}), {6}: (17, {}),... | custom-call | flops 146028888064 | bytes 94371840 | tf_op jit(solution)/shard_map/pallas_call | solution.py:411
  628.0 113.0 %shard_map.327 = (bf16[2048,1024]{1,0:T(8,128)(2,1)}, f32[2048,1024]{1,0:T(8,128)}, bf16[2048,1024]{1,0:T(8,128)(2,1)}, bf16[8192,1024]{1,0:T(8,128)(2,1)}, bf16...) custom-call(s32[5]{0:T(128)} %get-tuple-element.213.refs_0_, ...), custom_call_target="tpu_custom_call", output_to_operand_aliasing={{3}: (14, {}), {4}: (15, {}), {5}: (16, {}), {6}: (17, {}),... | custom-call | flops 146028888064 | bytes 94371840 | tf_op jit(solution)/shard_map/pallas_call | solution.py:411
  741.0 82.3 %shard_map.336 = f32[2,2,2,512,1024]{4,3,2,1,0:T(8,128)} custom-call(s32[5]{0:T(128)} %get-tuple-element.215.refs_0_, bf16[8192,1024]{1,0:T(8,128)(2,1)} %get-tuple-element.167.refs_1_, bf16[8192,4096]{1,0:T(8,128)(2,1)} %get-tuple-element.168.refs_2_), custom_call_target="tpu_custom_call" | custom-call | flops 68719476736 | bytes 134217728 | tf_op jit(solution)/shard_map/pallas_call | solution.py:411
  823.4 53.7 %shard_map.328 = (bf16[2048,1024]{1,0:T(8,128)(2,1)}, bf16[8192,3072]{1,0:T(8,128)(2,1)}, f32[2,8,1024]{2,1,0:T(8,128)}, f32[1024,128]{1,0:T(8,128)}, f32[2,8,1024]{2,1,0:T(8,128)}) custom-call(s32[5]{0:T(128)} %get-tuple-element.212.refs_0_, s32[128]{0:T(128)} %refs_1_.9, ...), custom_call_target="tpu_custom_call", output_to_operand_aliasing={{1}: (18, {})} | custom-call | flops 98784247808 | bytes 52428800 | tf_op jit(solution)/shard_map/pallas_call | solution.py:411
  878.1 91.5 %collective-permute-done.22.refs_5_ = bf16[2048,1024]{1,0:T(8,128)(2,1)} collective-permute-done((bf16[2048,1024]{1,0:T(8,128)(2,1)}, bf16[2048,1024]{1,0:T(8,128)(2,1)}, u32[]{:S(2)}, u32[]{:S(2)}) %collective-permute-start.22) | collective-permute-done | bytes 4194336 | tf_op jit(solution)/shard_map/ppermute | solution.py:425
  977.1 91.7 %shard_map.332 = (f32[2,2,2,1024,512]{4,3,2,1,0:T(8,128)}, bf16[32768,1024]{1,0:T(8,128)(2,1)}) custom-call(s32[5]{0:T(128)} %stack.44.refs_0_, bf16[8192,4096]{1,0:T(8,128)(2,1)} %get-tuple-element.155.refs_1_, bf16[32768,1024]{1,0:T(8,128)(2,1)} %bitcast.8.refs_3_.refs_2_, ...), custom_call_target="tpu_custom_call", output_to_operand_aliasing={{1}: (7, {})} | custom-call | flops 68719476736 | bytes 134217728 | tf_op jit(solution)/shard_map/pallas_call | solution.py:411
  1070.9 91.7 %collective-permute-done.7.refs_21_ = bf16[2048,1024]{1,0:T(8,128)(2,1)} collective-permute-done((bf16[2048,1024]{1,0:T(8,128)(2,1)}, bf16[2048,1024]{1,0:T(8,128)(2,1)}, u32[]{:S(2)}, u32[]{:S(2)}) %collective-permute-start.7) | collective-permute-done | bytes 4194336 | tf_op jit(solution)/shard_map/ppermute | solution.py:425
  1166.3 86.3 %collective-permute-done.10.refs_21_ = bf16[2048,1024]{1,0:T(8,128)(2,1)} collective-permute-done((bf16[2048,1024]{1,0:T(8,128)(2,1)}, bf16[2048,1024]{1,0:T(8,128)(2,1)}, u32[]{:S(2)}, u32[]{:S(2)}) %collective-permute-start.10) | collective-permute-done | bytes 4194336 | tf_op jit(solution)/shard_map/ppermute | solution.py:425
  1252.6 55.5 %shard_map.329 = (bf16[2048,1024]{1,0:T(8,128)(2,1)}, bf16[8192,3072]{1,0:T(8,128)(2,1)}, f32[2,8,1024]{2,1,0:T(8,128)}, f32[1024,128]{1,0:T(8,128)}, f32[2,8,10...) custom-call(s32[5]{0:T(128)} %stack.42.refs_0_, s32[128]{0:T(128)} %refs_1_.9, ...), custom_call_target="tpu_custom_call", output_to_operand_aliasing={{1}: (18, {}), {5}: (23, {})} | custom-call | flops 98784247808 | bytes 52428800 | tf_op jit(solution)/shard_map/pallas_call | solution.py:411
  1308.1 33.5 %collective-permute-done.13.refs_5_ = bf16[2048,1024]{1,0:T(8,128)(2,1)} collective-permute-done((bf16[2048,1024]{1,0:T(8,128)(2,1)}, bf16[2048,1024]{1,0:T(8,128)(2,1)}, u32[]{:S(2)}, u32[]{:S(2)}) %collective-permute-start.13) | collective-permute-done | bytes 4194336 | tf_op jit(solution)/shard_map/ppermute | solution.py:425
  1341.6 55.8 %shard_map.330 = (bf16[2048,1024]{1,0:T(8,128)(2,1)}, bf16[8192,3072]{1,0:T(8,128)(2,1)}, f32[2,8,1024]{2,1,0:T(8,128)}, f32[1024,128]{1,0:T(8,128)}, f32[2,8,10...) custom-call(s32[5]{0:T(128)} %stack.36.refs_0_, s32[128]{0:T(128)} %refs_1_.9, ...), custom_call_target="tpu_custom_call", output_to_operand_aliasing={{1}: (18, {}), {5}: (23, {})} | custom-call | flops 98784247808 | bytes 52428800 | tf_op jit(solution)/shard_map/pallas_call | solution.py:411
  1397.4 52.0 %shard_map.331 = (f32[2,2,2,2,512,256]{5,4,3,2,1,0:T(8,128)}, bf16[32768,1024]{1,0:T(8,128)(2,1)}) custom-call(s32[5]{0:T(128)} %stack.32.refs_0_, bf16[8192,1024]{1,0:T(8,128)(2,1)} %get-tuple-element.94.refs_1_, bf16[8192,3072]{1,0:T(8,128)(2,1)} %get-tuple-element.148.refs_2_, ...), custom_call_target="tpu_custom_call", output_to_operand_aliasing={{1}: (7, {})} | custom-call | flops 34359738368 | bytes 67108864 | tf_op jit(solution)/shard_map/pallas_call | solution.py:411
  1451.0 91.8 %collective-permute-done.19.refs_5_ = bf16[2048,1024]{1,0:T(8,128)(2,1)} collective-permute-done((bf16[2048,1024]{1,0:T(8,128)(2,1)}, bf16[2048,1024]{1,0:T(8,128)(2,1)}, u32[]{:S(2)}, u32[]{:S(2)}) %collective-permute-start.19) | collective-permute-done | bytes 4194336 | tf_op jit(solution)/shard_map/ppermute | solution.py:425
  1544.6 27.0 %shard_map.335 = f32[2,2,2,512,256]{4,3,2,1,0:T(8,128)} custom-call(s32[5]{0:T(128)} %get-tuple-element.215.refs_0_, bf16[8192,1024]{1,0:T(8,128)(2,1)} %get-tuple-element.94.refs_1_, bf16[8192,3072]{1,0:T(8,128)(2,1)} %get-tuple-element.148.refs_2_), custom_call_target="tpu_custom_call" | custom-call | flops 17179869184 | bytes 33554432 | tf_op jit(solution)/shard_map/pallas_call | solution.py:411
  1574.9 32.7 %shard_map.333 = (f32[2,2,2,256,512]{4,3,2,1,0:T(8,128)}, bf16[32768,1024]{1,0:T(8,128)(2,1)}) custom-call(s32[5]{0:T(128)} %stack.43.refs_0_, bf16[8192,1024]{1,0:T(8,128)(2,1)} %get-tuple-element.98.refs_2_.refs_1_, bf16[8192,1024]{1,0:T(8,128)(2,1)} %get-tuple-element.153.refs_2_, ...), custom_call_target="tpu_custom_call", output_to_operand_aliasing={{1}: (7, {})} | custom-call | flops 17179869184 | bytes 33554432 | tf_op jit(solution)/shard_map/pallas_call | solution.py:411
  1610.0 26.6 %collective-permute-done.16.refs_3_ = bf16[2048,1024]{1,0:T(8,128)(2,1)} collective-permute-done((bf16[2048,1024]{1,0:T(8,128)(2,1)}, bf16[2048,1024]{1,0:T(8,128)(2,1)}, u32[]{:S(2)}, u32[]{:S(2)}) %collective-permute-start.16) | collective-permute-done | bytes 4194336 | tf_op jit(solution)/shard_map/ppermute | solution.py:425
  1647.6 23.3 %collective-permute-done.25 = f32[13312]{0:T(1024)S(1)} collective-permute-done((f32[13312]{0:T(1024)S(1)}, f32[13312]{0:T(1024)S(1)}, u32[]{:S(2)}, u32[]{:S(2)}) %collective-permute-start.25) | collective-permute-done | bytes 53280 | tf_op jit(solution)/shard_map/ppermute | solution.py:638
  1717.7 86.5 %collective-permute-done.27 = f32[2,512,256]{1,2,0:T(8,128)} collective-permute-done((f32[2,512,256]{1,2,0:T(8,128)}, f32[2,512,256]{1,2,0:T(8,128)}, u32[]{:S(2)}, u32[]{:S(2)}) %collective-permute-start.27) | collective-permute-done | bytes 1048608 | tf_op jit(solution)/shard_map/ppermute | solution.py:562
  (218 shorter events, 126.7 us)
Async XLA Ops:
  9.7 188.1 %all-gather.10.cloned.1.call-start = ((), (), s32[]{:S(2)}) async-start(), calls=%async_computation.3 | async-start | bytes 2359296 | tf_op jit(solution)/shard_map/all_gather | solution.py:467
  10.5 187.3 %all-gather.14.cloned.1.call-start = ((), (), s32[]{:S(2)}) async-start(), calls=%async_computation.8 | async-start | bytes 9437184 | tf_op jit(solution)/shard_map/all_gather | solution.py:468
  11.2 186.6 %all-gather.16.cloned.1.call-start = ((), (), s32[]{:S(2)}) async-start(), calls=%async_computation.9 | async-start | bytes 9437184 | tf_op jit(solution)/shard_map/all_gather | solution.py:469
  11.8 1667.9 %reduce-scatter.6.cloned.1.call-start = ((), (), s32[]{:S(2)}) async-start(), calls=%async_computation.5 | async-start | bytes 20971520 | tf_op jit(solution)/shard_map/reduce_scatter | solution.py:567
  310.6 204.6 %collective-permute-start = (bf16[2048,1024]{1,0:T(8,128)(2,1)}, bf16[2048,1024]{1,0:T(8,128)(2,1)}, u32[]{:S(2)}, u32[]{:S(2)}) collective-permute-start(bf16[2048,1024]{1,0:T(8,128)(2,1)} %get-tuple-element.114.refs_18_), channel_id=1, source_target_pairs={{0,1},{1,0},{2,3},{3,2},{4,5},{5,4},{6,7},{7,6}} | collective-permute-start | bytes 12582920 | tf_op jit(solution)/shard_map/ppermute | solution.py:426
  310.9 93.8 %collective-permute-start.1 = (bf16[2048,1024]{1,0:T(8,128)(2,1)}, bf16[2048,1024]{1,0:T(8,128)(2,1)}, u32[]{:S(2)}, u32[]{:S(2)}) collective-permute-start(bf16[2048,1024]{1,0:T(8,128)(2,1)} %get-tuple-element.114.refs_18_), channel_id=1, source_target_pairs={{0,2},{2,0},{1,3},{3,1},{4,6},{6,4},{5,7},{7,5}} | collective-permute-start | bytes 12582920 | tf_op jit(solution)/shard_map/ppermute | solution.py:425
  367.6 260.4 %collective-permute-start.3 = (bf16[2048,1024]{1,0:T(8,128)(2,1)}, bf16[2048,1024]{1,0:T(8,128)(2,1)}, u32[]{:S(2)}, u32[]{:S(2)}) collective-permute-start(bf16[2048,1024]{1,0:T(8,128)(2,1)} %get-tuple-element.125.refs_18_), channel_id=1, source_target_pairs={{0,1},{1,0},{2,3},{3,2},{4,5},{5,4},{6,7},{7,6}} | collective-permute-start | bytes 12582920 | tf_op jit(solution)/shard_map/ppermute | solution.py:426
  367.7 147.0 %collective-permute-start.4 = (bf16[2048,1024]{1,0:T(8,128)(2,1)}, bf16[2048,1024]{1,0:T(8,128)(2,1)}, u32[]{:S(2)}, u32[]{:S(2)}) collective-permute-start(bf16[2048,1024]{1,0:T(8,128)(2,1)} %get-tuple-element.125.refs_18_), channel_id=1, source_target_pairs={{0,2},{2,0},{1,3},{3,1},{4,6},{6,4},{5,7},{7,5}} | collective-permute-start | bytes 12582920 | tf_op jit(solution)/shard_map/ppermute | solution.py:425
  404.6 110.6 %collective-permute-start.2 = (bf16[2048,1024]{1,0:T(8,128)(2,1)}, bf16[2048,1024]{1,0:T(8,128)(2,1)}, u32[]{:S(2)}, u32[]{:S(2)}) collective-permute-start(bf16[2048,1024]{1,0:T(8,128)(2,1)} %collective-permute-done.1.refs_20_), channel_id=1, source_target_pairs={{0,1},{1,0},{2,3},{3,2},{4,5},{5,4},{6,7},{7,6}} | collective-permute-start | bytes 12582920 | tf_op jit(solution)/shard_map/ppermute | solution.py:427
  514.7 113.3 %collective-permute-start.5 = (bf16[2048,1024]{1,0:T(8,128)(2,1)}, bf16[2048,1024]{1,0:T(8,128)(2,1)}, u32[]{:S(2)}, u32[]{:S(2)}) collective-permute-start(bf16[2048,1024]{1,0:T(8,128)(2,1)} %collective-permute-done.4.refs_20_), channel_id=1, source_target_pairs={{0,1},{1,0},{2,3},{3,2},{4,5},{5,4},{6,7},{7,6}} | collective-permute-start | bytes 12582920 | tf_op jit(solution)/shard_map/ppermute | solution.py:427
  823.4 860.7 %reduce-scatter.8.cloned.1.call-start = ((), (), s32[]{:S(2)}) async-start(), calls=%async_computation.6 | async-start | bytes 20971520 | tf_op jit(solution)/shard_map/reduce_scatter | solution.py:567
  1068.8 620.0 %reduce-scatter.4.cloned.1.call-start = ((), (), s32[]{:S(2)}) async-start(), calls=%async_computation.4 | async-start | bytes 10485760 | tf_op jit(solution)/shard_map/reduce_scatter | solution.py:567
  1068.9 93.8 %collective-permute-start.7 = (bf16[2048,1024]{1,0:T(8,128)(2,1)}, bf16[2048,1024]{1,0:T(8,128)(2,1)}, u32[]{:S(2)}, u32[]{:S(2)}) collective-permute-start(bf16[2048,1024]{1,0:T(8,128)(2,1)} %get-tuple-element.140.refs_19_), channel_id=1, source_target_pairs={{0,2},{2,0},{1,3},{3,1},{4,6},{6,4},{5,7},{7,5}} | collective-permute-start | bytes 12582920 | tf_op jit(solution)/shard_map/ppermute | solution.py:425
  1070.2 94.8 %collective-permute-start.6 = (bf16[2048,1024]{1,0:T(8,128)(2,1)}, bf16[2048,1024]{1,0:T(8,128)(2,1)}, u32[]{:S(2)}, u32[]{:S(2)}) collective-permute-start(bf16[2048,1024]{1,0:T(8,128)(2,1)} %get-tuple-element.140.refs_19_), channel_id=1, source_target_pairs={{0,1},{1,0},{2,3},{3,2},{4,5},{5,4},{6,7},{7,6}} | collective-permute-start | bytes 12582920 | tf_op jit(solution)/shard_map/ppermute | solution.py:426
  1070.2 182.4 %collective-permute-start.10 = (bf16[2048,1024]{1,0:T(8,128)(2,1)}, bf16[2048,1024]{1,0:T(8,128)(2,1)}, u32[]{:S(2)}, u32[]{:S(2)}) collective-permute-start(bf16[2048,1024]{1,0:T(8,128)(2,1)} %get-tuple-element.146.refs_19_), channel_id=1, source_target_pairs={{0,2},{2,0},{1,3},{3,1},{4,6},{6,4},{5,7},{7,5}} | collective-permute-start | bytes 12582920 | tf_op jit(solution)/shard_map/ppermute | solution.py:425
  1164.5 177.1 %collective-permute-start.9 = (bf16[2048,1024]{1,0:T(8,128)(2,1)}, bf16[2048,1024]{1,0:T(8,128)(2,1)}, u32[]{:S(2)}, u32[]{:S(2)}) collective-permute-start(bf16[2048,1024]{1,0:T(8,128)(2,1)} %get-tuple-element.146.refs_19_), channel_id=1, source_target_pairs={{0,1},{1,0},{2,3},{3,2},{4,5},{5,4},{6,7},{7,6}} | collective-permute-start | bytes 12582920 | tf_op jit(solution)/shard_map/ppermute | solution.py:426
  1165.0 232.4 %collective-permute-start.12 = (bf16[2048,1024]{1,0:T(8,128)(2,1)}, bf16[2048,1024]{1,0:T(8,128)(2,1)}, u32[]{:S(2)}, u32[]{:S(2)}) collective-permute-start(bf16[2048,1024]{1,0:T(8,128)(2,1)} %get-tuple-element.149.refs_3_), channel_id=1, source_target_pairs={{0,1},{1,0},{2,3},{3,2},{4,5},{5,4},{6,7},{7,6}} | collective-permute-start | bytes 12582920 | tf_op jit(solution)/shard_map/ppermute | solution.py:426
  1165.0 176.6 %collective-permute-start.13 = (bf16[2048,1024]{1,0:T(8,128)(2,1)}, bf16[2048,1024]{1,0:T(8,128)(2,1)}, u32[]{:S(2)}, u32[]{:S(2)}) collective-permute-start(bf16[2048,1024]{1,0:T(8,128)(2,1)} %get-tuple-element.149.refs_3_), channel_id=1, source_target_pairs={{0,2},{2,0},{1,3},{3,1},{4,6},{6,4},{5,7},{7,5}} | collective-permute-start | bytes 12582920 | tf_op jit(solution)/shard_map/ppermute | solution.py:425
  1449.5 93.3 %collective-permute-start.19 = (bf16[2048,1024]{1,0:T(8,128)(2,1)}, bf16[2048,1024]{1,0:T(8,128)(2,1)}, u32[]{:S(2)}, u32[]{:S(2)}) collective-permute-start(bf16[2048,1024]{1,0:T(8,128)(2,1)} %get-tuple-element.154.refs_3_), channel_id=1, source_target_pairs={{0,2},{2,0},{1,3},{3,1},{4,6},{6,4},{5,7},{7,5}} | collective-permute-start | bytes 12582920 | tf_op jit(solution)/shard_map/ppermute | solution.py:425
  1450.8 124.1 %collective-permute-start.18 = (bf16[2048,1024]{1,0:T(8,128)(2,1)}, bf16[2048,1024]{1,0:T(8,128)(2,1)}, u32[]{:S(2)}, u32[]{:S(2)}) collective-permute-start(bf16[2048,1024]{1,0:T(8,128)(2,1)} %get-tuple-element.154.refs_3_), channel_id=1, source_target_pairs={{0,1},{1,0},{2,3},{3,2},{4,5},{5,4},{6,7},{7,6}} | collective-permute-start | bytes 12582920 | tf_op jit(solution)/shard_map/ppermute | solution.py:426
  1543.4 93.3 %collective-permute-start.16 = (bf16[2048,1024]{1,0:T(8,128)(2,1)}, bf16[2048,1024]{1,0:T(8,128)(2,1)}, u32[]{:S(2)}, u32[]{:S(2)}) collective-permute-start(bf16[2048,1024]{1,0:T(8,128)(2,1)} %get-tuple-element.152.refs_1_), channel_id=1, source_target_pairs={{0,2},{2,0},{1,3},{3,1},{4,6},{6,4},{5,7},{7,5}} | collective-permute-start | bytes 12582920 | tf_op jit(solution)/shard_map/ppermute | solution.py:425
  1682.8 123.8 %collective-permute-start.34 = (f32[512,1024]{1,0:T(8,128)}, f32[512,1024]{1,0:T(8,128)}, u32[]{:S(2)}, u32[]{:S(2)}) collective-permute-start(f32[512,1024]{1,0:T(8,128)} %dynamic-slice_bitcast_fusion.1), channel_id=1, source_target_pairs={{0,2},{2,0},{1,3},{3,1},{4,6},{6,4},{5,7},{7,5}} | collective-permute-start | bytes 6291464 | tf_op jit(solution)/shard_map/ppermute | solution.py:562
  1687.9 122.7 %collective-permute-start.35 = (f32[1024,512]{1,0:T(8,128)}, f32[1024,512]{1,0:T(8,128)}, u32[]{:S(2)}, u32[]{:S(2)}) collective-permute-start(f32[1024,512]{1,0:T(8,128)} %dynamic-slice_bitcast_fusion), channel_id=1, source_target_pairs={{0,2},{2,0},{1,3},{3,1},{4,6},{6,4},{5,7},{7,5}} | collective-permute-start | bytes 6291464 | tf_op jit(solution)/shard_map/ppermute | solution.py:562
  1693.9 110.3 %collective-permute-start.27 = (f32[2,512,256]{1,2,0:T(8,128)}, f32[2,512,256]{1,2,0:T(8,128)}, u32[]{:S(2)}, u32[]{:S(2)}) collective-permute-start(f32[2,512,256]{1,2,0:T(8,128)} %bitcast.106), channel_id=1, source_target_pairs={{0,2},{2,0},{1,3},{3,1},{4,6},{6,4},{5,7},{7,5}} | collective-permute-start | bytes 3145736 | tf_op jit(solution)/shard_map/ppermute | solution.py:562
  (40 other events, 1198.8 us)
Sparse Core Ops, SparseCore 0:
  10.5 43.3 all-gather.11
  55.6 22.2 all-gather.9
  79.7 48.6 all-gather.13
  130.1 48.6 all-gather.15
  823.5 119.7 reduce-scatter.5
  1069.0 121.6 reduce-scatter.7
  1449.6 67.8 reduce-scatter.3
